TPU v7x, 32 devices: a whole 2x2x4 slice. The times are simulated.
32 devices in a mesh: member: 2 (over x), band: 16 (over z, y, core).
Axes of the slice: x: 2, y: 2, z: 4, core: 2. Of those that a mesh axis runs over, the one named last changes fastest.
Arguments:
- grid_in: bfloat16 [32, 274, 5248], P(('member', 'band')), parts along dimension 0, may hold values from -6 to 6
- legendre: bfloat16 [16, 2, 640, 8], P('band'), may hold values from -2 to 2
- gauss_weight: float32 [8], replicated, may hold values from 0.2 to 2
- vertical_modes: float32 [137, 137], replicated
- coupling: float32 [137, 137], replicated, may hold values from -0.5 to 0.5
- mode_rates: float32 [137], replicated, may hold values from 0.1 to 10
- loop_length: int32 [16], replicated, may hold values from 20 to 5136, as said below
- lat_order: int32 [16], replicated, may hold values from 0 to 15, each once
- wave_number: int32 [16], replicated, may hold values from 0 to 1279, as said below
Outputs:
- grid_out: bfloat16 [32, 274, 5248], P(('member', 'band')), parts along dimension 0
There are 2 independent parts, one for each index of `member`. A program takes and returns all parts, laid end to end along the dimension named above; an argument that names none is the same for every part. Nothing has to cross between parts.
Inputs may be any that keep to these rules, and one draw needn't show every extreme that they name: loop_length[t] = 20 + 4 k with k not falling from the poles toward the equator, equal for latitudes t and 15 - t; the equatorial loops have 5248 - 112 points. Row i of grid_in and grid_out holds latitude lat_order[i]. `wave_number`: distinct values.
All inputs are finite; a program needn't handle non-finite values.
Results may differ from a plain program's by a relative error of at most 0.013.
Values may be sent and summed in bfloat16 or wider, within the bound.
A program may use at most 64 MiB of HBM per device.

v0:
```python
import math

import jax
import jax.numpy as jnp
from jax import lax
from jax.sharding import PartitionSpec as P

TRUNC = 1279


implicit_step = 0.5
highest = lax.Precision.HIGHEST


def loop_tables(length, wave_list, block_count):
    offsets = jnp.arange(128, dtype=jnp.int32)
    inner_turn = offsets[:, None] * wave_list[None, :] % length
    angles = inner_turn.astype(jnp.float32) * (2.0 * math.pi) / length.astype(jnp.float32)
    inner_table = jnp.concatenate([jnp.cos(angles), jnp.sin(angles)], axis=1).astype(jnp.bfloat16)
    block_index = jnp.arange(block_count, dtype=jnp.int32)
    outer_turn = block_index[:, None] * 128 * wave_list[None, :] % length
    phases = outer_turn.astype(jnp.float32) * (2.0 * math.pi) / length.astype(jnp.float32)
    return (inner_table, jnp.cos(phases), jnp.sin(phases))


def forward_loop(one_loop, length, wave_list):
    field_count, loop_width = one_loop.shape
    block_count = loop_width // 128
    wave_count = wave_list.shape[0]
    inner_table, cos_turn, sin_turn = loop_tables(length, wave_list, block_count)
    inside = jnp.arange(loop_width, dtype=jnp.int32) < length
    masked = jnp.where(inside[None, :], one_loop, jnp.zeros((), one_loop.dtype))
    products = jnp.dot(
        masked.reshape(field_count * block_count, 128),
        inner_table,
        preferred_element_type=jnp.float32,
    )
    products = products.reshape(field_count, block_count, 2, wave_count)
    real_part = jnp.sum(cos_turn * products[:, :, 0] - sin_turn * products[:, :, 1], axis=1)
    imag_part = -jnp.sum(sin_turn * products[:, :, 0] + cos_turn * products[:, :, 1], axis=1)
    inverse_len = 1.0 / length.astype(jnp.float32)
    together = jnp.concatenate([real_part, imag_part], axis=0) * inverse_len
    resolved = 2 * wave_list < length
    together = jnp.where(resolved[None, :], together, 0.0)
    return together.T.astype(jnp.bfloat16)


def inverse_loop(fourier, length, wave_list, loop_width):
    block_count = loop_width // 128
    wave_count = wave_list.shape[0]
    field_count = fourier.shape[1] // 2
    inner_table, cos_turn, sin_turn = loop_tables(length, wave_list, block_count)
    doubling = jnp.where(wave_list == 0, 1.0, 2.0).astype(jnp.float32)
    real_part = fourier[:, :field_count].astype(jnp.float32).T * doubling
    imag_part = fourier[:, field_count:].astype(jnp.float32).T * doubling
    cosine_part = real_part[:, None, :] * cos_turn[None] - imag_part[:, None, :] * sin_turn[None]
    sine_part = -(real_part[:, None, :] * sin_turn[None] + imag_part[:, None, :] * cos_turn[None])
    combined = jnp.concatenate([cosine_part, sine_part], axis=2).astype(jnp.bfloat16)
    points = lax.dot_general(
        combined.reshape(field_count * block_count, 2 * wave_count),
        inner_table,
        (((1,), (1,)), ((), ())),
        preferred_element_type=jnp.float32,
    )
    points = points.reshape(field_count, loop_width)
    inside = jnp.arange(loop_width, dtype=jnp.int32) < length
    return jnp.where(inside[None, :], points, 0.0).astype(jnp.bfloat16)


def semi_implicit(spectral, wave_values, vertical_modes, coupling, mode_rates):
    half_rows = spectral.shape[-2]
    level_count = vertical_modes.shape[0]
    parity = jnp.arange(2, dtype=jnp.int32)
    row_index = jnp.arange(half_rows, dtype=jnp.int32)
    degree = wave_values[..., None, None] + parity[:, None] + 2 * row_index[None, :]
    kept_rows = degree <= TRUNC
    spectral = jnp.where(kept_rows[..., None], spectral, 0.0)
    damping = (degree * (degree + 1)).astype(jnp.float32) / float(TRUNC * (TRUNC + 1))
    reshaped = spectral.reshape(spectral.shape[:-1] + (2, 2, level_count))
    divergence = reshaped[..., 0, :]
    pressure = reshaped[..., 1, :]
    factor_e = damping[..., None, None]
    right_side = divergence - implicit_step * factor_e * jnp.einsum(
        "...l,kl->...k", pressure, coupling, precision=highest
    )
    in_modes = jnp.einsum("...l,lk->...k", right_side, vertical_modes, precision=highest)
    in_modes = in_modes / (1.0 + implicit_step * factor_e * mode_rates)
    new_div = jnp.einsum("...k,lk->...l", in_modes, vertical_modes, precision=highest)
    new_press = pressure - implicit_step * jnp.einsum(
        "...l,kl->...k", new_div, coupling, precision=highest
    )
    updated = jnp.stack([new_div, new_press], axis=-2)
    return updated.reshape(spectral.shape).astype(jnp.bfloat16)


def per_device(
    grid_in,
    legendre,
    gauss_weight,
    vertical_modes,
    coupling,
    mode_rates,
    loop_length,
    lat_order,
    wave_number,
):
    groups = lax.axis_size("band")
    band_index = lax.axis_index("band")
    loop_count, field_count, loop_width = grid_in.shape
    slot_count = legendre.shape[0]
    lat_count = lat_order.shape[0]
    half_count = lat_count // 2
    column_count = 2 * field_count
    wave_total = wave_number.shape[0]
    own_rows = lax.dynamic_slice_in_dim(lat_order, band_index * loop_count, loop_count)
    own_lengths = jnp.take(loop_length, own_rows)
    column_waves = wave_number.reshape(groups, slot_count).T.reshape(wave_total)
    own_waves = lax.dynamic_slice_in_dim(wave_number, band_index * slot_count, slot_count)

    def forward_piece(scan_carry, scan_item):
        one_loop, length = scan_item
        loop_piece = forward_loop(one_loop, length, column_waves).reshape(
            slot_count, groups, column_count
        )
        return (
            scan_carry,
            lax.all_to_all(loop_piece, "band", split_axis=1, concat_axis=1, tiled=True),
        )

    unused, pieces = lax.scan(forward_piece, 0, (grid_in, own_lengths))
    arrived = jnp.transpose(pieces, (1, 2, 0, 3))
    arrived = arrived.reshape(slot_count, lat_count, column_count)
    row_of_lat = jnp.argsort(lat_order)
    northern = jnp.take(arrived, row_of_lat[:half_count], axis=1).astype(jnp.float32)
    southern = jnp.take(arrived, row_of_lat[::-1][:half_count], axis=1).astype(jnp.float32)
    weight = gauss_weight[None, :, None]
    even_part = (weight * (northern + southern)).astype(jnp.bfloat16)
    odd_part = (weight * (northern - southern)).astype(jnp.bfloat16)
    stacked = jnp.stack([even_part, odd_part], axis=1)
    spectral = jnp.einsum("kprj,kpjc->kprc", legendre, stacked, preferred_element_type=jnp.float32)
    updated = semi_implicit(spectral, own_waves, vertical_modes, coupling, mode_rates)
    summed = jnp.einsum("kprj,kprc->kpjc", legendre, updated, preferred_element_type=jnp.float32)
    northern_back = summed[:, 0] + summed[:, 1]
    southern_back = summed[:, 0] - summed[:, 1]
    by_lat = jnp.concatenate([northern_back, southern_back[:, ::-1]], axis=1)
    resolved = 2 * own_waves[:, None] < loop_length[None, :]
    by_lat = jnp.where(resolved[:, :, None], by_lat, 0.0).astype(jnp.bfloat16)
    returning = jnp.take(by_lat, lat_order, axis=1).reshape(
        slot_count, groups, loop_count, column_count
    )
    outgoing_loops = jnp.transpose(returning, (2, 0, 1, 3))

    def inverse_piece(scan_carry, scan_item):
        loop_data, length = scan_item
        loop_back = lax.all_to_all(loop_data, "band", split_axis=1, concat_axis=1, tiled=True)
        return (
            scan_carry,
            inverse_loop(
                loop_back.reshape(wave_total, column_count), length, column_waves, loop_width
            ),
        )

    unused, grid_out = lax.scan(inverse_piece, 0, (outgoing_loops, own_lengths))
    return grid_out


def solution(mesh):
    placed = (
        P(("member", "band"), None, None),
        P("band", None, None, None),
        P(),
        P(),
        P(),
        P(),
        P(),
        P(),
        P(),
    )
    return jax.shard_map(
        per_device,
        mesh=mesh,
        in_specs=placed,
        out_specs=P(("member", "band"), None, None),
        check_vma=False,
    )
```

profile of v0, /device:TPU:0, one launch (start us, length us, event | category | flops | bytes accessed | tf_op | source)
XLA Modules:
  0.0 72.8 jit_solution(2726533253867949105)
XLA Ops:
  0.0 1.3 %dynamic_slice.17 = s32[1]{0:T(128)} dynamic-slice(s32[16]{0:T(128)} %param.18, s32[]{:T(128)S(6)} %select_n.129), dynamic_slice_sizes={1} | dynamic-slice | bytes 12 | tf_op jit(solution)/shard_map/dynamic_slice | solution.py:115
  3.2 1.3 %dynamic-slice.3 = s32[1]{0:T(128)} dynamic-slice(s32[16]{0:T(128)} %param.17, s32[]{:T(128)} %bitcast), dynamic_slice_sizes={1} | dynamic-slice | bytes 12 | tf_op jit(solution)/shard_map/jit(_take)/gather | solution.py:116
  5.8 3.7 %broadcast_select_fusion = bf16[1,274,5248]{2,1,0:T(8,128)(2,1)} fusion(bf16[1,274,5248]{2,1,0:T(8,128)(2,1)} %param.11, pred[5248]{0:T(1024)(128)(4,1)S(1)} %iota_compare_fusion), kind=kLoop, calls=%fused_computation.6 | loop fusion | flops 1437952 | bytes 5757056 | tf_op jit(solution)/shard_map/while/body/eval_jaxpr/jit(_where)/select_n | solution.py:32
  9.4 4.2 %select_n.136 = bf16[274,41,128]{2,1,0:T(8,128)(2,1)S(1)} reshape(bf16[1,274,5248]{2,1,0:T(8,128)(2,1)} %broadcast_select_fusion) | data formatting | bytes 5751808 | tf_op jit(solution)/shard_map/while/body/eval_jaxpr/jit(_where)/select_n | solution.py:32
  14.4 1.1 %fusion.46 = (f32[41,16]{1,0:T(8,128)S(1)}, f32[41,16]{1,0:T(8,128)S(1)}) fusion(f32[]{:T(128)S(6)} %convert_element_type.103, pred[]{:T(512)S(6)} %lt.94, s32[]{:T(128)S(6)} %select_n.133, s32[16]{0:T(128)} %param.19, s32[41]{0:T(128)} %iota_multiply_fusion.1), kind=kLoop, calls=%fused_computation.77 | loop fusion | flops 7216 | bytes 5485 | tf_op jit(solution)/shard_map/while/body/eval_jaxpr/cos | solution.py:23
  15.5 1.6 %fusion = f32[274,41,2,16]{0,3,2,1:T(8,128)S(1)} fusion(bf16[2,16,128,1]{2,1,0,3:T(8,128)(2,1)S(1)} %bitcast.133, bf16[274,41,128,1]{2,1,0,3:T(8,128)(2,1)S(1)} %bitcast.123), kind=kOutput, calls=%fused_computation.4 | convolution fusion | flops 92028928 | bytes 4322048 | tf_op jit(solution)/shard_map/while/body/eval_jaxpr/dot_general | solution.py:33
  18.4 0.7 reduce
  19.1 0.7 reshape.543
  19.8 7.4 %all-to-all-start = ((bf16[16,2,274]{2,1,0:T(2,128)(2,1)}), bf16[16,2,274]{2,1,0:T(2,128)(2,1)S(1)}, u32[]{:S(2)}, u32[]{:S(2)}) async-start(bf16[16,2,274]{2,1,0:T(2,128)(2,1)} %reshape.543), calls=%async_computation | async-start | bytes 49152 | tf_op jit(solution)/shard_map/while/body/eval_jaxpr/all_to_all | solution.py:127
  27.2 1.3 %sort.17 = (s32[16]{0:T(128)}, s32[16]{0:T(128)S(1)}) sort(s32[16]{0:T(128)S(1)} %copy-done.10, s32[16]{0:T(128)S(1)} %iota.42), dimensions={0}, to_apply=%region_2.3 | sort | flops 64 | bytes 256 | tf_op jit(solution)/shard_map/jit(argsort)/sort | solution.py:133
  28.7 0.7 dynamic_slice.18
  29.4 0.7 iota_add_fusion
  31.1 2.6 %all-to-all-done = bf16[16,2,274]{2,1,0:T(2,128)(2,1)S(1)} async-done(((bf16[16,2,274]{2,1,0:T(2,128)(2,1)}), bf16[16,2,274]{2,1,0:T(2,128)(2,1)S(1)}, u32[]{:S(2)}, u32[]{:S(2)}) %all-to-all-start) | async-done | bytes 17568 | tf_op jit(solution)/shard_map/while/body/eval_jaxpr/all_to_all | solution.py:127
  35.1 0.6 select_bitcast_fusion
  35.8 1.4 %copy.35 = f32[2,640,548]{1,0,2:T(2,128)S(1)} copy(f32[2,640,548]{1,2,0:T(8,128)S(1)} %select_bitcast_fusion) | data formatting | bytes 5611520 | tf_op jit(solution)/shard_map/jit(_where)/select_n | solution.py:77
  37.2 1.0 %fusion.60 = (f32[1,2,640,2,1,137]{2,1,5,4,3,0:T(2,128)S(1)}, f32[1,2,640,2,1,137]{2,1,5,4,3,0:T(2,128)S(1)}) fusion(f32[1,2,640,2,2,137]{2,1,5,4,3,0:T(2,128)S(1)} %bitcast.124), kind=kLoop, calls=%fused_computation.115 | loop fusion | bytes 5611520 | tf_op jit(solution)/shard_map/slice | solution.py:81
  38.2 1.4 %fusion.8 = f32[2,640,2,137]{1,3,2,0:T(8,128)S(1)} fusion(f32[1,2,640,2,1,137]{2,1,5,4,3,0:T(2,128)S(1)} %get-tuple-element.53, f32[137,137]{1,0:T(8,128)S(1)} %copy-done.1), kind=kOutput, calls=%fused_computation.17 | convolution fusion | flops 576583680 | bytes 2880836 | tf_op jit(solution)/shard_map/...l,kl->...k/dot_general | solution.py:83
  39.7 1.6 %fusion.3 = f32[2,640,2,137]{1,3,2,0:T(8,128)S(1)} fusion(f32[1,2,640,2,1,137]{2,1,5,4,3,0:T(2,128)S(1)} %get-tuple-element.54, f32[2,640,2,137]{1,3,2,0:T(8,128)S(1)} %fusion.8, f32[2,640]{1,0:T(2,128)S(1)} %fusion.57, f32[137,137]{1,0:T(8,128)S(1)} %copy-done), kind=kOutput, calls=%fused_computation.12 | convolution fusion | flops 577285120 | bytes 4288836 | tf_op jit(solution)/shard_map/...l,lk->...k/dot_general | solution.py:86
  41.3 1.6 %fusion.5 = f32[2,640,2,137]{1,3,2,0:T(8,128)S(1)} fusion(f32[2,640,2,137]{1,3,2,0:T(8,128)S(1)} %fusion.3, f32[2,640,137]{1,2,0:T(8,128)S(1)} %multiply_add_fusion, f32[137,137]{1,0:T(8,128)S(1)} %copy-done), kind=kOutput, calls=%fused_computation.14 | convolution fusion | flops 576934400 | bytes 3582276 | tf_op jit(solution)/shard_map/...k,lk->...l/dot_general | solution.py:88
  43.0 1.5 %fusion.11 = bf16[1,2,640,2,1,137]{2,5,3,1,4,0:T(8,128)(2,1)S(1)} fusion(f32[2,640,2,137]{1,3,2,0:T(8,128)S(1)} %fusion.5, f32[1,2,640,2,1,137]{2,1,5,4,3,0:T(2,128)S(1)} %get-tuple-element.53, f32[137,137]{1,0:T(8,128)S(1)} %copy-done.1), kind=kOutput, calls=%fused_computation.20 | convolution fusion | flops 577635840 | bytes 3582276 | tf_op jit(solution)/shard_map/...l,kl->...k/dot_general | solution.py:89
  44.7 1.1 %copy.39 = bf16[1,2,640,2,2,137]{2,1,5,4,3,0:T(2,128)(2,1)S(1)} copy(bf16[1,2,640,2,2,137]{2,5,3,1,4,0:T(8,128)(2,1)S(1)} %pad_maximum_fusion) | data formatting | bytes 2805760 | tf_op jit(solution)/shard_map/stack | solution.py:92
  47.2 0.7 reduce.1
  47.9 0.7 reshape.545
  48.6 3.7 %all-to-all-start.1 = ((bf16[16,2,274]{2,1,0:T(2,128)(2,1)}), bf16[16,2,274]{2,1,0:T(2,128)(2,1)S(1)}, u32[]{:S(2)}, u32[]{:S(2)}) async-start(bf16[16,2,274]{2,1,0:T(2,128)(2,1)} %reshape.545), calls=%async_computation.1 | async-start | bytes 49152 | tf_op jit(solution)/shard_map/while/body/eval_jaxpr/all_to_all | solution.py:155
  52.3 6.3 %all-to-all-done.1 = bf16[16,2,274]{2,1,0:T(2,128)(2,1)S(1)} async-done(((bf16[16,2,274]{2,1,0:T(2,128)(2,1)}), bf16[16,2,274]{2,1,0:T(2,128)(2,1)S(1)}, u32[]{:S(2)}, u32[]{:S(2)}) %all-to-all-start.1) | async-done | bytes 17568 | tf_op jit(solution)/shard_map/while/body/eval_jaxpr/all_to_all | solution.py:155
  59.2 0.9 %copy.43 = bf16[274,41,16]{1,0,2:T(8,128)(2,1)S(1)} copy(bf16[274,41,16]{0,2,1:T(8,128)(2,1)S(1)} %get-tuple-element.56) | data formatting | bytes 718976 | tf_op jit(solution)/shard_map/convert.2
  60.1 0.7 neg.14
  60.7 0.9 %copy.42 = bf16[274,41,16]{1,0,2:T(8,128)(2,1)S(1)} copy(bf16[274,41,16]{0,2,1:T(8,128)(2,1)S(1)} %get-tuple-element.55) | data formatting | bytes 718976 | tf_op jit(solution)/shard_map/convert.3
  61.6 0.7 sub.44
  62.3 3.3 %fusion.17 = bf16[11234,128]{1,0:T(8,128)(2,1)} fusion(bf16[11234,16]{0,1:T(8,128)(2,1)S(1)} %neg.14, bf16[11234,16]{0,1:T(8,128)(2,1)S(1)} %sub.44, bf16[128,16]{0,1:T(8,128)(2,1)S(1)} %get-tuple-element.66, bf16[128,16]{0,1:T(8,128)(2,1)S(1)} %get-tuple-element.65), kind=kOutput, calls=%fused_computation.32 | convolution fusion | flops 93483264 | bytes 3603072 | tf_op jit(solution)/shard_map/while/body/eval_jaxpr/dot_general | solution.py:59
  65.6 5.2 %reshape.469 = bf16[1,274,5248]{2,1,0:T(8,128)(2,1)S(1)} reshape(bf16[11234,128]{1,0:T(8,128)(2,1)} %fusion.17) | data formatting | bytes 5751808 | tf_op jit(solution)/shard_map/while/body/eval_jaxpr/reshape | solution.py:65
  70.7 2.1 %select_convert_fusion = bf16[1,274,5248]{2,1,0:T(8,128)(2,1)} fusion(bf16[1,274,5248]{2,1,0:T(8,128)(2,1)S(1)} %reshape.469, pred[5248]{0:T(1024)(128)(4,1)S(1)} %iota_compare_fusion), kind=kLoop, calls=%fused_computation.3 | loop fusion | flops 1437952 | bytes 5757056 | tf_op jit(solution)/shard_map/while/body/eval_jaxpr/convert_element_type | solution.py:67
  (68 shorter events, 6.5 us)
Async XLA Ops:
  0.0 39.7 %copy-start = (f32[137,137]{1,0:T(8,128)S(1)}, f32[137,137]{1,0:T(8,128)}, u32[]{:S(2)}) copy-start(f32[137,137]{1,0:T(8,128)} %param.14) | copy-start | bytes 225232
  9.4 4.2 %copy-start.5 = (s32[16]{0:T(128)S(1)}, s32[16]{0:T(128)}, u32[]{:S(2)}) copy-start(s32[16]{0:T(128)} %param.19) | copy-start | bytes 196
  15.5 1.7 %copy-start.2 = (f32[41,16]{1,0:T(8,128)}, f32[41,16]{1,0:T(8,128)S(1)}, u32[]{:S(2)}) copy-start(f32[41,16]{1,0:T(8,128)S(1)} %get-tuple-element.64) | copy-start | bytes 7876
  17.1 0.7 copy-start.9
  17.1 10.1 %copy-start.10 = (s32[16]{0:T(128)S(1)}, s32[16]{0:T(128)}, u32[]{:S(2)}) copy-start(s32[16]{0:T(128)} %param.18) | copy-start | bytes 196
  17.1 11.6 %copy-start.6 = (s32[16]{0:T(128)S(1)}, s32[16]{0:T(128)}, u32[]{:S(2)}) copy-start(s32[16]{0:T(128)} %param.19) | copy-start | bytes 196
  17.1 13.8 %copy-start.11 = (s32[16]{0:T(128)S(1)}, s32[16]{0:T(128)}, u32[]{:S(2)}) copy-start(s32[16]{0:T(128)} %param.17) | copy-start | bytes 196
  17.1 13.8 %copy-start.7 = (f32[137]{0:T(256)S(1)}, f32[137]{0:T(256)}, u32[]{:S(2)}) copy-start(f32[137]{0:T(256)} %param.16) | copy-start | bytes 1648
  17.2 17.9 %copy-start.8 = (f32[8]{0:T(128)S(1)}, f32[8]{0:T(128)}, u32[]{:S(2)}) copy-start(f32[8]{0:T(128)} %param.13) | copy-start | bytes 100
  17.2 17.9 %copy-start.4 = (bf16[1,2,640,8]{2,3,1,0:T(8,128)(2,1)S(1)}, bf16[1,2,640,8]{2,3,1,0:T(8,128)(2,1)}, u32[]{:S(2)}) copy-start(bf16[1,2,640,8]{2,3,1,0:T(8,128)(2,1)} %param.12) | copy-start | bytes 61444
  19.8 14.0 %all-to-all-start = ((bf16[16,2,274]{2,1,0:T(2,128)(2,1)}), bf16[16,2,274]{2,1,0:T(2,128)(2,1)S(1)}, u32[]{:S(2)}, u32[]{:S(2)}) async-start(bf16[16,2,274]{2,1,0:T(2,128)(2,1)} %reshape.543), calls=%async_computation | async-start | bytes 49152 | tf_op jit(solution)/shard_map/while/body/eval_jaxpr/all_to_all | solution.py:127
  37.2 1.0 %copy-start.1 = (f32[137,137]{1,0:T(8,128)S(1)}, f32[137,137]{1,0:T(8,128)}, u32[]{:S(2)}) copy-start(f32[137,137]{1,0:T(8,128)} %param.15) | copy-start | bytes 225232
  45.8 13.0 %copy-start.3 = (f32[41,16]{1,0:T(8,128)S(1)}, f32[41,16]{1,0:T(8,128)}, u32[]{:S(2)}) copy-start(f32[41,16]{1,0:T(8,128)} %copy-done.2) | copy-start | bytes 7876
  48.6 10.0 %all-to-all-start.1 = ((bf16[16,2,274]{2,1,0:T(2,128)(2,1)}), bf16[16,2,274]{2,1,0:T(2,128)(2,1)S(1)}, u32[]{:S(2)}, u32[]{:S(2)}) async-start(bf16[16,2,274]{2,1,0:T(2,128)(2,1)} %reshape.545), calls=%async_computation.1 | async-start | bytes 49152 | tf_op jit(solution)/shard_map/while/body/eval_jaxpr/all_to_all | solution.py:155
where the time goes:
time: 73.4 us; the launch traced here: 72.8 us
  local copies, waits for them, and re-layouts  23.6 us (32%)
  other arithmetic  13.2 us (18%)
  matrix products  12.1 us (16%)
  starting transfers between devices  11.1 us (15%)
  waiting for transfers between devices  8.92 us (12%)
  between operations  3.86 us (5%)
    all_to_all x1, starting transfers between devices, forward_piece(): lax.all_to_all(loop_piece, 'band', split_axis=1, concat_axis=1, tiled=True)  7.42 us
    all_to_all x1, waiting for transfers between devices, inverse_piece(): lax.all_to_all(loop_data, 'band', split_axis=1, concat_axis=1, tiled=True)  6.3 us
    reshape x1, local copies, waits for them, and re-layouts, inverse_loop(): points = points.reshape(field_count, loop_width)  5.17 us
    select_n x1, local copies, waits for them, and re-layouts, forward_loop(): masked = jnp.where(inside[None, :], one_loop, jnp.zeros((), one_loop.dtype))  4.15 us
    all_to_all x1, starting transfers between devices, inverse_piece(): lax.all_to_all(loop_data, 'band', split_axis=1, concat_axis=1, tiled=True)  3.72 us
    select_n x1, other arithmetic, forward_loop(): masked = jnp.where(inside[None, :], one_loop, jnp.zeros((), one_loop.dtype))  3.66 us
    dot_general x1, matrix products, inverse_loop(): lax.dot_general(combined.reshape(field_count * block_count, 2 * wave_coun...  3.28 us
    all_to_all x1, waiting for transfers between devices, forward_piece(): lax.all_to_all(loop_piece, 'band', split_axis=1, concat_axis=1, tiled=True)  2.62 us
  transfers between devices with their start and end apart: 2, of which 2 were waited for; matrix products, arithmetic and copies ran while one was open for 4% of the time, Pallas kernels for 0%

commit v1 on v0

v1 whole, which is shorter than its diff:
```python
import functools
import math

import jax
import jax.numpy as jnp
from jax import lax
from jax.experimental import pallas as pl
from jax.experimental.pallas import tpu as pltpu
from jax.sharding import PartitionSpec as P

TRUNC = 1279
STEP = 0.5
F32 = jnp.float32
BF16 = jnp.bfloat16
HIGHEST = lax.Precision.HIGHEST
NT = (((1,), (1,)), ((), ()))
NN = (((1,), (0,)), ((), ()))
TN = (((0,), (0,)), ((), ()))


def dot(a, b, dims=NN, precision=None):
    return lax.dot_general(a, b, dims, precision=precision, preferred_element_type=F32)


def iota(shape, dim):
    return lax.broadcasted_iota(jnp.int32, shape, dim)


def sin_cos(turns, quarter_shift):
    quarter = jnp.floor(4.0 * turns + 0.5)
    y = (turns - 0.25 * quarter) * (2.0 * math.pi)
    z = y * y
    sine = y + y * z * (-1.6666654611e-1 + z * (8.3321608736e-3 + z * (-1.9515295891e-4)))
    cosine = 1.0 - 0.5 * z + z * z * (4.166664568298827e-2 + z * (-1.388731625493765e-3 + z * 2.443315711809948e-5))
    k = quarter.astype(jnp.int32) - quarter_shift
    swap = (k & 1) == 1
    cos_sign = jnp.where(((k + 1) & 2) == 0, 1.0, -1.0)
    sin_sign = jnp.where((k & 2) == 0, 1.0, -1.0)
    return (
        cos_sign * jnp.where(swap, sine, cosine),
        sin_sign * jnp.where(swap, cosine, sine),
    )


def spread(values, index, start):
    out = jnp.full(index.shape, start, F32)
    for at, value in enumerate(values):
        out = jnp.where(index == at, value, out)
    return out


def chunk_bounds(blocks, pieces):
    edges = [blocks * i // pieces for i in range(pieces + 1)]
    return [(a * 128, b * 128) for a, b in zip(edges[:-1], edges[1:]) if b > a]


def main_kernel(
    groups,
    chunks,
    grid_hbm,
    leg_ref,
    gauss_ref,
    modes_ref,
    coupling_ref,
    rates_ref,
    length_ref,
    order_ref,
    wave_ref,
    coef_ref,
    table_ref,
    grid_vmem,
    wf_ref,
    wb_ref,
    mu_ref,
    send_one,
    recv_one,
    send_two,
    recv_two,
    in_sem,
    ssem_one,
    rsem_one,
    ssem_two,
    rsem_two,
):
    me = lax.axis_index("band")
    field_count, width = grid_vmem.shape
    levels = modes_ref.shape[0]
    half_rows, nh = leg_ref.shape[2], leg_ref.shape[3]
    lats = order_ref.shape[0]
    rows = 2 * groups
    kpad = wb_ref.shape[1]

    loads = []
    for at, (lo, hi) in enumerate(chunks):
        copy = pltpu.make_async_copy(
            grid_hbm.at[0, :, lo:hi], grid_vmem.at[:, lo:hi], in_sem.at[at]
        )
        copy.start()
        loads.append(copy)

    barrier = pltpu.get_barrier_semaphore()

    def each_peer(body):
        if groups <= 16:
            for step in range(1, groups):
                body(lax.rem(me + step, groups))
        else:

            def step_body(step, carry):
                body(lax.rem(me + step, groups))
                return carry

            lax.fori_loop(1, groups, step_body, 0)

    each_peer(lambda peer: pl.semaphore_signal(barrier, inc=1, device_id={"band": peer}))

    length = length_ref[order_ref[me]]
    length_f = length.astype(F32)
    row_id = iota((rows, 128), 0)
    lane_id = iota((rows, 128), 1)
    row_q = row_id & 1
    wave_rows = spread([wave_ref[d].astype(F32) for d in range(groups)], row_id >> 1, 0.0)
    inverse_len = 1.0 / jnp.full((rows, 128), length_f, F32)

    def turns_of(product):
        return (product - jnp.floor(product * inverse_len + 0.5) * length_f) * inverse_len

    inner_c, inner_s = sin_cos(turns_of(wave_rows * lane_id.astype(F32)), row_q)
    outer_c, outer_s = sin_cos(turns_of(wave_rows * (lane_id * 128).astype(F32)), 0)
    scale = jnp.where(2.0 * wave_rows < length_f, inverse_len, 0.0)
    scale = jnp.where(row_q == 0, scale, -scale)[:, :1]
    for a in range(width // 128):
        block = outer_c[:, a : a + 1] * inner_c - outer_s[:, a : a + 1] * inner_s
        block = jnp.where(lane_id < length - 128 * a, block, 0.0)
        table_ref[:, a * 128 : (a + 1) * 128] = block.astype(BF16)

    total = jnp.zeros((rows, field_count), F32)
    for copy, (lo, hi) in zip(loads, chunks):
        copy.wait()
        total += dot(table_ref[:, lo:hi], grid_vmem[:, lo:hi], NT)
    fourier = total * scale

    def exchange(values, send, recv, ssem, rsem):
        packed = values.astype(BF16)
        for d in range(groups):
            send[d] = packed[2 * d : 2 * d + 2, :]

        def start(peer):
            pltpu.make_async_remote_copy(
                src_ref=send.at[peer],
                dst_ref=recv.at[me],
                send_sem=ssem.at[peer],
                recv_sem=rsem.at[me],
                device_id={"band": peer},
            ).start()

        def finish(peer):
            copy = pltpu.make_async_remote_copy(
                src_ref=send.at[peer],
                dst_ref=recv.at[peer],
                send_sem=ssem.at[peer],
                recv_sem=rsem.at[peer],
                device_id={"band": peer},
            )
            copy.wait_recv()
            copy.wait_send()

        return start, finish

    start, finish = exchange(fourier, send_one, recv_one, ssem_one, rsem_one)
    pl.semaphore_wait(barrier, groups - 1)
    each_peer(start)
    recv_one[me] = send_one[me]

    modes = modes_ref[...]
    coupling = coupling_ref[...]
    wf_ref[...] = jnp.zeros(wf_ref.shape, F32)
    wb_ref[...] = jnp.zeros(wb_ref.shape, F32)
    mu_ref[...] = jnp.zeros(mu_ref.shape, F32)
    mu_ref[:, 0:levels] = rates_ref[...].reshape(1, levels)
    wf_ref[0:levels, 0:levels] = modes
    wf_ref[levels : 2 * levels, kpad : kpad + levels] = dot(coupling, modes, TN, HIGHEST)
    wb_ref[0:levels, 0:levels] = modes
    wb_ref[levels : 2 * levels, 0:levels] = -STEP * dot(coupling, modes, NN, HIGHEST)
    wf = wf_ref[...].astype(BF16)
    wb = wb_ref[...].astype(BF16)

    wave = wave_ref[me]
    order = [order_ref[i] for i in range(lats)]
    order_f = [o.astype(F32) for o in order]
    gauss = [gauss_ref[jnp.minimum(o, lats - 1 - o)] for o in order]
    solved = [jnp.where(2 * wave < length_ref[o], 1.0, 0.0) for o in order]
    boost = jnp.where(wave == 0, 1.0, 2.0)

    lane_one = iota((1, 2 * rows), 1)
    lane_row = jnp.where(lane_one < rows, lane_one, lane_one - rows)
    lane_lat = spread(order_f, lane_row >> 1, 0.0)
    lane_gauss = spread(gauss, lane_row >> 1, 0.0)
    north_j = iota((nh, 2 * rows), 0).astype(F32)
    col_row = iota((rows, nh), 0)
    col_lat = spread(order_f, col_row >> 1, 0.0)
    col_scale = spread(solved, iota((rows, 1), 0) >> 1, 0.0) * boost
    col_scale = jnp.where((iota((rows, 1), 0) & 1) == 0, col_scale, -col_scale)
    col_j = iota((rows, nh), 1).astype(F32)

    denom = float(TRUNC * (TRUNC + 1))
    m_parts, lt_parts, g_parts = [], [], []
    for p in range(2):
        leg = leg_ref[0, p]
        degree = wave + p + 2 * iota((half_rows, 1), 0)
        damp = (degree * (degree + 1)).astype(F32) * (STEP / denom)
        degree_lane = wave + p + 2 * iota((1, half_rows), 1)
        kept = jnp.where(degree_lane <= TRUNC, 1.0, 0.0)
        g_parts.append(1.0 / (1.0 + damp * mu_ref[...]))
        sign = 1.0 if p == 0 else -1.0
        pick_lane = jnp.where(lane_lat == north_j, 1.0, 0.0) + jnp.where(
            lane_lat == (lats - 1) - north_j, sign, 0.0
        )
        pick_col = jnp.where(col_lat == col_j, 1.0, 0.0) + jnp.where(
            col_lat == (lats - 1) - col_j, sign, 0.0
        )
        weight = jnp.where(lane_one < rows, 1.0, -damp) * lane_gauss
        for q in range(2):
            chosen = jnp.where((lane_one & 1) == q, pick_lane, 0.0).astype(BF16)
            m_parts.append((dot(leg, chosen) * weight).astype(BF16))
            chosen = jnp.where((col_row & 1) == q, pick_col, 0.0).astype(BF16)
            lt_parts.append((dot(chosen, leg, NT) * kept * col_scale).astype(BF16))
    through = sum(dot(lt, m) for lt, m in zip(lt_parts, m_parts))[:, 0:rows].astype(BF16)

    each_peer(finish)
    arrived = recv_one[...].reshape(rows, field_count)
    in_modes = dot(arrived, wf).astype(BF16)
    stacked = jnp.concatenate([in_modes[:, :kpad], in_modes[:, kpad:]], axis=0)
    passed = dot(through, arrived)
    back = jnp.zeros((rows, kpad), F32)
    for at in range(4):
        solved_part = (dot(m_parts[at], stacked) * g_parts[at // 2]).astype(BF16)
        back += dot(lt_parts[at], solved_part)
    result = dot(back.astype(BF16), wb, NT)
    result += jnp.where(iota((rows, field_count), 1) >= levels, passed, 0.0)

    start, finish = exchange(result, send_two, recv_two, ssem_two, rsem_two)
    each_peer(start)
    recv_two[me] = send_two[me]
    each_peer(finish)
    coef_ref[...] = recv_two[...].reshape(rows, field_count)


def inverse_kernel(coef_ref, table_ref, out_ref):
    out_ref[0] = dot(coef_ref[...], table_ref[...], TN).astype(BF16)


def per_device(
    groups,
    grid_in,
    legendre,
    gauss_weight,
    vertical_modes,
    coupling,
    mode_rates,
    loop_length,
    lat_order,
    wave_number,
):
    loop_count, field_count, width = grid_in.shape
    assert loop_count == 1 and legendre.shape[0] == 1
    rows = 2 * groups
    levels = vertical_modes.shape[0]
    kpad = -(-levels // 128) * 128
    chunks = chunk_bounds(width // 128, 8)
    vmem = pl.BlockSpec(memory_space=pltpu.VMEM)
    smem = pl.BlockSpec(memory_space=pltpu.SMEM)
    slot = pltpu.VMEM((groups, 2, field_count), BF16)
    sems = pltpu.SemaphoreType.DMA((groups,))
    coef, table = pl.pallas_call(
        functools.partial(main_kernel, groups, chunks),
        out_shape=(
            jax.ShapeDtypeStruct((rows, field_count), BF16),
            jax.ShapeDtypeStruct((rows, width), BF16),
        ),
        in_specs=[pl.BlockSpec(memory_space=pl.ANY), vmem, smem, vmem, vmem, vmem, smem, smem, smem],
        out_specs=(vmem, vmem),
        scratch_shapes=[
            pltpu.VMEM((field_count, width), BF16),
            pltpu.VMEM((2 * levels, 2 * kpad), F32),
            pltpu.VMEM((2 * levels, kpad), F32),
            pltpu.VMEM((1, kpad), F32),
            slot,
            slot,
            slot,
            slot,
            pltpu.SemaphoreType.DMA((len(chunks),)),
            sems,
            sems,
            sems,
            sems,
        ],
        compiler_params=pltpu.CompilerParams(
            collective_id=0, has_side_effects=True, vmem_limit_bytes=32 * 1024 * 1024
        ),
        name="forward_spectral",
    )(
        grid_in,
        legendre,
        gauss_weight,
        vertical_modes,
        coupling,
        mode_rates,
        loop_length,
        lat_order,
        wave_number,
    )
    tile = 640
    return pl.pallas_call(
        inverse_kernel,
        grid=(-(-width // tile),),
        out_shape=jax.ShapeDtypeStruct(grid_in.shape, BF16),
        in_specs=[
            pl.BlockSpec((rows, field_count), lambda i: (0, 0)),
            pl.BlockSpec((rows, tile), lambda i: (0, i)),
        ],
        out_specs=pl.BlockSpec((1, field_count, tile), lambda i: (0, 0, i)),
        compiler_params=pltpu.CompilerParams(vmem_limit_bytes=32 * 1024 * 1024),
        name="inverse",
    )(coef, table)


def solution(mesh):
    groups = mesh.shape["band"]
    placed = (
        P(("member", "band"), None, None),
        P("band", None, None, None),
        P(),
        P(),
        P(),
        P(),
        P(),
        P(),
        P(),
    )
    return jax.shard_map(
        functools.partial(per_device, groups),
        mesh=mesh,
        in_specs=placed,
        out_specs=P(("member", "band"), None, None),
        check_vma=False,
    )
```

time: 73.4 us -> 29.9 us (0.41)
  Pallas kernels: 0 us -> 21.7 us
  local copies, waits for them, and re-layouts: 23.6 us -> 7.88 us
  other arithmetic: 13.2 us -> 0 us
  matrix products: 12.1 us -> 0 us
  starting transfers between devices: 11.1 us -> 0 us
  waiting for transfers between devices: 8.92 us -> 0 us
  between operations: 3.86 us -> 0.03 us
    pallas_call x0 -> x2, Pallas kernels: none -> 21.7 us  [the longest x1 16.6 us: per_device(): pl.pallas_call(functools.partial(main_kernel, groups, chunks), out_shape=...]
    dot_general x8 -> x0, matrix products: 12.1 us -> none  [the longest x1 3.28 us: inverse_loop(): lax.dot_general(combined.reshape(field_count * block_count, 2 * wave_coun...]
    all_to_all x2 -> x0, starting transfers between devices: 11.1 us -> none  [the longest x1 7.42 us: forward_piece(): lax.all_to_all(loop_piece, 'band', split_axis=1, concat_axis=1, tiled=True)]
    all_to_all x2 -> x0, waiting for transfers between devices: 8.92 us -> none  [the longest x1 6.3 us: inverse_piece(): lax.all_to_all(loop_data, 'band', split_axis=1, concat_axis=1, tiled=True)]
    select_n x3 -> x0, local copies, waits for them, and re-layouts: 5.63 us -> none  [the longest x1 4.15 us: forward_loop(): masked = jnp.where(inside[None, :], one_loop, jnp.zeros((), one_loop.dtype))]
    unnamed x31 -> x17, local copies, waits for them, and re-layouts: 2.35 us -> 7.88 us
    reshape x2 -> x0, local copies, waits for them, and re-layouts: 5.2 us -> none  [the longest x1 5.17 us: inverse_loop(): points = points.reshape(field_count, loop_width)]
    select_n x5 -> x0, other arithmetic: 3.75 us -> none  [the longest x1 3.66 us: forward_loop(): masked = jnp.where(inside[None, :], one_loop, jnp.zeros((), one_loop.dtype))]
  transfers between devices with their start and end apart: 2 -> 0, of which waited for: 2 -> 0; matrix products, arithmetic and copies ran while one was open for 4% -> 0% of each run, Pallas kernels for 0% -> 0%
where the time goes in v1:
time: 29.9 us; the launch traced here: 29.6 us
  Pallas kernels  21.7 us (73%)
  local copies, waits for them, and re-layouts  7.88 us (26%)
    pallas_call x1, Pallas kernels, per_device(): pl.pallas_call(functools.partial(main_kernel, groups, chunks), out_shape=...  16.6 us
    unnamed x17, local copies, waits for them, and re-layouts  7.88 us
    pallas_call x1, Pallas kernels, per_device(): pl.pallas_call(inverse_kernel, grid=(-(-width // tile),), out_shape=jax.S...  5.08 us

profile of v1, /device:TPU:0, one launch (start us, length us, event | category | flops | bytes accessed | tf_op | source)
XLA Modules:
  0.0 29.6 jit_solution(1754395098257791233)
XLA Ops:
  0.0 0.9 %copy.10.leg_ref = bf16[1,2,640,8]{3,2,1,0:T(8,128)(2,1)S(1)} copy(bf16[1,2,640,8]{2,3,1,0:T(8,128)(2,1)} %param.10) | data formatting | bytes 40960 | tf_op args[1]
  0.9 0.0 copy-start
  1.0 1.8 %copy-done = bf16[1,274,5248]{2,1,0:T(8,128)(2,1)S(1)} copy-done((bf16[1,274,5248]{2,1,0:T(8,128)(2,1)S(1)}, bf16[1,274,5248]{2,1,0:T(8,128)(2,1)}, u32[]{:S(2)}) %copy-start) | copy-done | bytes 2875928
  2.8 0.0 copy-start.1
  2.8 0.9 %copy-done.1 = f32[137,137]{1,0:T(8,128)S(1)} copy-done((f32[137,137]{1,0:T(8,128)S(1)}, f32[137,137]{1,0:T(8,128)}, u32[]{:S(2)}) %copy-start.1) | copy-done | bytes 75100
  3.7 0.0 copy-start.2
  3.7 0.9 %copy-done.2 = f32[137,137]{1,0:T(8,128)S(1)} copy-done((f32[137,137]{1,0:T(8,128)S(1)}, f32[137,137]{1,0:T(8,128)}, u32[]{:S(2)}) %copy-start.2) | copy-done | bytes 75100
  4.6 0.0 copy-start.3
  4.6 0.7 %copy-done.3 = f32[137]{0:T(256)S(1)} copy-done((f32[137]{0:T(256)S(1)}, f32[137]{0:T(256)}, u32[]{:S(2)}) %copy-start.3) | copy-done | bytes 572
  5.3 0.0 copy-start.4
  5.3 0.7 %copy-done.4 = f32[8]{0:T(128)S(1)} copy-done((f32[8]{0:T(128)S(1)}, f32[8]{0:T(128)}, u32[]{:S(2)}) %copy-start.4) | copy-done | bytes 56
  5.9 0.0 copy-start.5
  5.9 0.7 %copy-done.5 = s32[16]{0:T(128)S(1)} copy-done((s32[16]{0:T(128)S(1)}, s32[16]{0:T(128)}, u32[]{:S(2)}) %copy-start.5) | copy-done | bytes 88
  6.6 0.0 copy-start.6
  6.6 0.7 %copy-done.6 = s32[16]{0:T(128)S(1)} copy-done((s32[16]{0:T(128)S(1)}, s32[16]{0:T(128)}, u32[]{:S(2)}) %copy-start.6) | copy-done | bytes 88
  7.2 0.0 copy-start.7
  7.3 0.7 %copy-done.7 = s32[16]{0:T(128)S(1)} copy-done((s32[16]{0:T(128)S(1)}, s32[16]{0:T(128)}, u32[]{:S(2)}) %copy-start.7) | copy-done | bytes 88
  7.9 16.6 %forward_spectral.1 = (bf16[32,274]{1,0:T(8,128)(2,1)S(1)}, bf16[32,5248]{1,0:T(8,128)(2,1)S(1)}) custom-call(bf16[1,274,5248]{2,1,0:T(8,128)(2,1)S(1)} %copy-done, bf16[1,2,640,8]{3,2,1,0:T(8,128)(2,1)S(1)} %copy.10.leg_ref, f32[8]{0:T(128)S(1)} %copy-done.4, f32[137,137]{1,0:T(8,128)S(1)} %copy-done.1, f32[137,137]{1,0:T(8,128)S(1)} %copy-done.2, ...), custom_call_target="tpu_custom_call" | custom-call | tf_op jit(solution)/shard_map/forward_spectral/pallas_call | solution.py:275
  24.6 5.1 %inverse.1 = bf16[1,274,5248]{2,1,0:T(8,128)(2,1)} custom-call(bf16[32,274]{1,0:T(8,128)(2,1)S(1)} %get-tuple-element.7.coef_ref, bf16[32,5248]{1,0:T(8,128)(2,1)S(1)} %get-tuple-element.8.table_ref), custom_call_target="tpu_custom_call" | custom-call | tf_op jit(solution)/shard_map/inverse/pallas_call | solution.py:314
Async XLA Ops:
  0.9 1.8 %copy-start = (bf16[1,274,5248]{2,1,0:T(8,128)(2,1)S(1)}, bf16[1,274,5248]{2,1,0:T(8,128)(2,1)}, u32[]{:S(2)}) copy-start(bf16[1,274,5248]{2,1,0:T(8,128)(2,1)} %grid_hbm.1) | copy-start | bytes 8627716
  2.8 0.9 %copy-start.1 = (f32[137,137]{1,0:T(8,128)S(1)}, f32[137,137]{1,0:T(8,128)}, u32[]{:S(2)}) copy-start(f32[137,137]{1,0:T(8,128)} %modes_ref.1) | copy-start | bytes 225232
  3.7 0.9 %copy-start.2 = (f32[137,137]{1,0:T(8,128)S(1)}, f32[137,137]{1,0:T(8,128)}, u32[]{:S(2)}) copy-start(f32[137,137]{1,0:T(8,128)} %coupling_ref.1) | copy-start | bytes 225232
  4.6 0.7 %copy-start.3 = (f32[137]{0:T(256)S(1)}, f32[137]{0:T(256)}, u32[]{:S(2)}) copy-start(f32[137]{0:T(256)} %rates_ref.1) | copy-start | bytes 1648
  5.3 0.7 %copy-start.4 = (f32[8]{0:T(128)S(1)}, f32[8]{0:T(128)}, u32[]{:S(2)}) copy-start(f32[8]{0:T(128)} %gauss_ref.1) | copy-start | bytes 100
  5.9 0.7 %copy-start.5 = (s32[16]{0:T(128)S(1)}, s32[16]{0:T(128)}, u32[]{:S(2)}) copy-start(s32[16]{0:T(128)} %length_ref.1) | copy-start | bytes 196
  6.6 0.7 %copy-start.6 = (s32[16]{0:T(128)S(1)}, s32[16]{0:T(128)}, u32[]{:S(2)}) copy-start(s32[16]{0:T(128)} %order_ref.1) | copy-start | bytes 196
  7.2 0.7 %copy-start.7 = (s32[16]{0:T(128)S(1)}, s32[16]{0:T(128)}, u32[]{:S(2)}) copy-start(s32[16]{0:T(128)} %wave_ref.1) | copy-start | bytes 196

commit v2 on v1

--- a/solution.py
+++ b/solution.py
@@ -58,6 +58,17 @@
     groups,
     chunks,
     grid_hbm,
+    leg_hbm,
+    gauss_hbm,
+    modes_hbm,
+    coupling_hbm,
+    rates_hbm,
+    length_hbm,
+    order_hbm,
+    wave_hbm,
+    coef_ref,
+    table_ref,
+    grid_vmem,
     leg_ref,
     gauss_ref,
     modes_ref,
@@ -66,9 +77,6 @@
     length_ref,
     order_ref,
     wave_ref,
-    coef_ref,
-    table_ref,
-    grid_vmem,
     wf_ref,
     wb_ref,
     mu_ref,
@@ -77,6 +85,7 @@
     send_two,
     recv_two,
     in_sem,
+    small_sem,
     ssem_one,
     rsem_one,
     ssem_two,
@@ -85,11 +94,28 @@
     me = lax.axis_index("band")
     field_count, width = grid_vmem.shape
     levels = modes_ref.shape[0]
-    half_rows, nh = leg_ref.shape[2], leg_ref.shape[3]
+    nh, half_rows = leg_ref.shape[2], leg_ref.shape[3]
     lats = order_ref.shape[0]
     rows = 2 * groups
     kpad = wb_ref.shape[1]
 
+    scalars = []
+    smalls = []
+    for at, (source, target) in enumerate(
+        (
+            (order_hbm, order_ref),
+            (length_hbm, length_ref),
+            (wave_hbm, wave_ref),
+            (gauss_hbm, gauss_ref),
+            (leg_hbm, leg_ref),
+            (modes_hbm, modes_ref),
+            (coupling_hbm, coupling_ref),
+            (rates_hbm, rates_ref),
+        )
+    ):
+        copy = pltpu.make_async_copy(source, target, small_sem.at[at])
+        copy.start()
+        (scalars if at < 4 else smalls).append(copy)
     loads = []
     for at, (lo, hi) in enumerate(chunks):
         copy = pltpu.make_async_copy(
@@ -113,6 +139,9 @@
             lax.fori_loop(1, groups, step_body, 0)
 
     each_peer(lambda peer: pl.semaphore_signal(barrier, inc=1, device_id={"band": peer}))
+
+    for copy in scalars:
+        copy.wait()
 
     length = length_ref[order_ref[me]]
     length_f = length.astype(F32)
@@ -172,6 +201,8 @@
     each_peer(start)
     recv_one[me] = send_one[me]
 
+    for copy in smalls:
+        copy.wait()
     modes = modes_ref[...]
     coupling = coupling_ref[...]
     wf_ref[...] = jnp.zeros(wf_ref.shape, F32)
@@ -222,9 +253,9 @@
         weight = jnp.where(lane_one < rows, 1.0, -damp) * lane_gauss
         for q in range(2):
             chosen = jnp.where((lane_one & 1) == q, pick_lane, 0.0).astype(BF16)
-            m_parts.append((dot(leg, chosen) * weight).astype(BF16))
+            m_parts.append((dot(leg, chosen, TN) * weight).astype(BF16))
             chosen = jnp.where((col_row & 1) == q, pick_col, 0.0).astype(BF16)
-            lt_parts.append((dot(chosen, leg, NT) * kept * col_scale).astype(BF16))
+            lt_parts.append((dot(chosen, leg) * kept * col_scale).astype(BF16))
     through = sum(dot(lt, m) for lt, m in zip(lt_parts, m_parts))[:, 0:rows].astype(BF16)
 
     each_peer(finish)
@@ -269,7 +300,7 @@
     kpad = -(-levels // 128) * 128
     chunks = chunk_bounds(width // 128, 8)
     vmem = pl.BlockSpec(memory_space=pltpu.VMEM)
-    smem = pl.BlockSpec(memory_space=pltpu.SMEM)
+    flipped = jnp.swapaxes(legendre, 2, 3)
     slot = pltpu.VMEM((groups, 2, field_count), BF16)
     sems = pltpu.SemaphoreType.DMA((groups,))
     coef, table = pl.pallas_call(
@@ -278,10 +309,18 @@
             jax.ShapeDtypeStruct((rows, field_count), BF16),
             jax.ShapeDtypeStruct((rows, width), BF16),
         ),
-        in_specs=[pl.BlockSpec(memory_space=pl.ANY), vmem, smem, vmem, vmem, vmem, smem, smem, smem],
+        in_specs=[pl.BlockSpec(memory_space=pltpu.HBM)] * 9,
         out_specs=(vmem, vmem),
         scratch_shapes=[
             pltpu.VMEM((field_count, width), BF16),
+            pltpu.VMEM(flipped.shape, BF16),
+            pltpu.SMEM(gauss_weight.shape, F32),
+            pltpu.VMEM(vertical_modes.shape, F32),
+            pltpu.VMEM(coupling.shape, F32),
+            pltpu.VMEM(mode_rates.shape, F32),
+            pltpu.SMEM(loop_length.shape, jnp.int32),
+            pltpu.SMEM(lat_order.shape, jnp.int32),
+            pltpu.SMEM(wave_number.shape, jnp.int32),
             pltpu.VMEM((2 * levels, 2 * kpad), F32),
             pltpu.VMEM((2 * levels, kpad), F32),
             pltpu.VMEM((1, kpad), F32),
@@ -290,6 +329,7 @@
             slot,
             slot,
             pltpu.SemaphoreType.DMA((len(chunks),)),
+            pltpu.SemaphoreType.DMA((8,)),
             sems,
             sems,
             sems,
@@ -300,15 +340,20 @@
         ),
         name="forward_spectral",
     )(
-        grid_in,
-        legendre,
-        gauss_weight,
-        vertical_modes,
-        coupling,
-        mode_rates,
-        loop_length,
-        lat_order,
-        wave_number,
+        *[
+            pltpu.with_memory_space_constraint(x, pltpu.HBM)
+            for x in (
+                grid_in,
+                flipped,
+                gauss_weight,
+                vertical_modes,
+                coupling,
+                mode_rates,
+                loop_length,
+                lat_order,
+                wave_number,
+            )
+        ]
     )
     tile = 640
     return pl.pallas_call(

time: 29.9 us -> 21.2 us (0.71)
  local copies, waits for them, and re-layouts: 7.88 us -> 0 us
  Pallas kernels: 21.7 us -> 21 us
    unnamed x17 -> x0, local copies, waits for them, and re-layouts: 7.88 us -> none
    pallas_call x1, Pallas kernels: 16.6 us -> 16 us  [per_device(): pl.pallas_call(functools.partial(main_kernel, groups, chunks), out_shape=...]
where the time goes in v2:
time: 21.2 us; the launch traced here: 21 us
  Pallas kernels  21 us (99%)
    pallas_call x1, Pallas kernels, per_device(): pl.pallas_call(functools.partial(main_kernel, groups, chunks), out_shape=...  16 us
    pallas_call x1, Pallas kernels, per_device(): pl.pallas_call(inverse_kernel, grid=(-(-width // tile),), out_shape=jax.S...  5.08 us

profile of v2, /device:TPU:0, one launch (start us, length us, event | category | flops | bytes accessed | tf_op | source)
XLA Modules:
  0.0 21.0 jit_solution(9894564705286105774)
XLA Ops:
  0.0 16.0 %forward_spectral.1 = (bf16[32,274]{1,0:T(8,128)(2,1)S(1)}, bf16[32,5248]{1,0:T(8,128)(2,1)S(1)}) custom-call(bf16[1,274,5248]{2,1,0:T(8,128)(2,1)} %grid_hbm.1, bf16[1,2,8,640]{3,2,1,0:T(8,128)(2,1)} %bitcast.1, f32[8]{0:T(128)} %gauss_hbm.1, f32[137,137]{1,0:T(8,128)} %modes_hbm.1, f32[137,137]{1,0:T(8,128)} %coupling_hbm.1, f32[137]{0:T(256)} %rates_hbm.1, ...), custom_call_target="tpu_custom_call" | custom-call | tf_op jit(solution)/shard_map/forward_spectral/pallas_call | solution.py:306
  16.0 5.1 %inverse.1 = bf16[1,274,5248]{2,1,0:T(8,128)(2,1)} custom-call(bf16[32,274]{1,0:T(8,128)(2,1)S(1)} %get-tuple-element.7.coef_ref, bf16[32,5248]{1,0:T(8,128)(2,1)S(1)} %get-tuple-element.8.table_ref), custom_call_target="tpu_custom_call" | custom-call | tf_op jit(solution)/shard_map/inverse/pallas_call | solution.py:359

commit v3 on v2

--- a/solution.py
+++ b/solution.py
@@ -128,7 +128,7 @@
 
     def each_peer(body):
         if groups <= 16:
-            for step in range(1, groups):
+            for step in sorted(range(1, groups), key=lambda k: abs(2 * k - groups)):
                 body(lax.rem(me + step, groups))
         else:
 
@@ -178,28 +178,24 @@
             pltpu.make_async_remote_copy(
                 src_ref=send.at[peer],
                 dst_ref=recv.at[me],
-                send_sem=ssem.at[peer],
-                recv_sem=rsem.at[me],
+                send_sem=ssem,
+                recv_sem=rsem,
                 device_id={"band": peer},
             ).start()
 
-        def finish(peer):
-            copy = pltpu.make_async_remote_copy(
-                src_ref=send.at[peer],
-                dst_ref=recv.at[peer],
-                send_sem=ssem.at[peer],
-                recv_sem=rsem.at[peer],
-                device_id={"band": peer},
-            )
-            copy.wait_recv()
-            copy.wait_send()
-
-        return start, finish
-
-    start, finish = exchange(fourier, send_one, recv_one, ssem_one, rsem_one)
+        others = pltpu.make_async_remote_copy(
+            src_ref=send.at[0 : groups - 1],
+            dst_ref=recv.at[0 : groups - 1],
+            send_sem=ssem,
+            recv_sem=rsem,
+            device_id={"band": lax.rem(me + 1, groups)},
+        )
+        each_peer(start)
+        recv[me] = send[me]
+        return others
+
     pl.semaphore_wait(barrier, groups - 1)
-    each_peer(start)
-    recv_one[me] = send_one[me]
+    first = exchange(fourier, send_one, recv_one, ssem_one, rsem_one)
 
     for copy in smalls:
         copy.wait()
@@ -258,7 +254,7 @@
             lt_parts.append((dot(chosen, leg) * kept * col_scale).astype(BF16))
     through = sum(dot(lt, m) for lt, m in zip(lt_parts, m_parts))[:, 0:rows].astype(BF16)
 
-    each_peer(finish)
+    first.wait_recv()
     arrived = recv_one[...].reshape(rows, field_count)
     in_modes = dot(arrived, wf).astype(BF16)
     stacked = jnp.concatenate([in_modes[:, :kpad], in_modes[:, kpad:]], axis=0)
@@ -270,15 +266,23 @@
     result = dot(back.astype(BF16), wb, NT)
     result += jnp.where(iota((rows, field_count), 1) >= levels, passed, 0.0)
 
-    start, finish = exchange(result, send_two, recv_two, ssem_two, rsem_two)
-    each_peer(start)
-    recv_two[me] = send_two[me]
-    each_peer(finish)
+    second = exchange(result, send_two, recv_two, ssem_two, rsem_two)
+    first.wait_send()
+    second.wait_recv()
+    second.wait_send()
     coef_ref[...] = recv_two[...].reshape(rows, field_count)
 
 
-def inverse_kernel(coef_ref, table_ref, out_ref):
-    out_ref[0] = dot(coef_ref[...], table_ref[...], TN).astype(BF16)
+def inverse_kernel(chunks, coef_ref, table_ref, out_hbm, points, sem):
+    coef = coef_ref[...].astype(F32).T.astype(BF16)
+    stores = []
+    for at, (lo, hi) in enumerate(chunks):
+        points[:, lo:hi] = dot(coef, table_ref[:, lo:hi]).astype(BF16)
+        copy = pltpu.make_async_copy(points.at[:, lo:hi], out_hbm.at[0, :, lo:hi], sem.at[at])
+        copy.start()
+        stores.append(copy)
+    for copy in stores:
+        copy.wait()
 
 
 def per_device(
@@ -299,10 +303,10 @@
     levels = vertical_modes.shape[0]
     kpad = -(-levels // 128) * 128
     chunks = chunk_bounds(width // 128, 8)
+    stores = chunk_bounds(width // 128, 10)
     vmem = pl.BlockSpec(memory_space=pltpu.VMEM)
     flipped = jnp.swapaxes(legendre, 2, 3)
     slot = pltpu.VMEM((groups, 2, field_count), BF16)
-    sems = pltpu.SemaphoreType.DMA((groups,))
     coef, table = pl.pallas_call(
         functools.partial(main_kernel, groups, chunks),
         out_shape=(
@@ -330,10 +334,10 @@
             slot,
             pltpu.SemaphoreType.DMA((len(chunks),)),
             pltpu.SemaphoreType.DMA((8,)),
-            sems,
-            sems,
-            sems,
-            sems,
+            pltpu.SemaphoreType.DMA(()),
+            pltpu.SemaphoreType.DMA(()),
+            pltpu.SemaphoreType.DMA(()),
+            pltpu.SemaphoreType.DMA(()),
         ],
         compiler_params=pltpu.CompilerParams(
             collective_id=0, has_side_effects=True, vmem_limit_bytes=32 * 1024 * 1024
@@ -355,16 +359,15 @@
             )
         ]
     )
-    tile = 640
     return pl.pallas_call(
-        inverse_kernel,
-        grid=(-(-width // tile),),
+        functools.partial(inverse_kernel, stores),
         out_shape=jax.ShapeDtypeStruct(grid_in.shape, BF16),
-        in_specs=[
-            pl.BlockSpec((rows, field_count), lambda i: (0, 0)),
-            pl.BlockSpec((rows, tile), lambda i: (0, i)),
+        in_specs=[vmem, vmem],
+        out_specs=pl.BlockSpec(memory_space=pltpu.HBM),
+        scratch_shapes=[
+            pltpu.VMEM((field_count, width), BF16),
+            pltpu.SemaphoreType.DMA((len(stores),)),
         ],
-        out_specs=pl.BlockSpec((1, field_count, tile), lambda i: (0, 0, i)),
         compiler_params=pltpu.CompilerParams(vmem_limit_bytes=32 * 1024 * 1024),
         name="inverse",
     )(coef, table)

time: 21.2 us -> 17.8 us (0.84)
  Pallas kernels: 21 us -> 17.6 us
    pallas_call x1, Pallas kernels: 5.08 us -> 1.99 us  [per_device(): pl.pallas_call(functools.partial(inverse_kernel, stores), out_shape=jax.S...]
    pallas_call x1, Pallas kernels: 16 us -> 15.7 us  [per_device(): pl.pallas_call(functools.partial(main_kernel, groups, chunks), out_shape=...]
where the time goes in v3:
time: 17.8 us; the launch traced here: 17.7 us
  Pallas kernels  17.6 us (99%)
    pallas_call x1, Pallas kernels, per_device(): pl.pallas_call(functools.partial(main_kernel, groups, chunks), out_shape=...  15.7 us
    pallas_call x1, Pallas kernels, per_device(): pl.pallas_call(functools.partial(inverse_kernel, stores), out_shape=jax.S...  1.99 us

profile of v3, /device:TPU:0, one launch (start us, length us, event | category | flops | bytes accessed | tf_op | source)
XLA Modules:
  0.0 17.7 jit_solution(17885813065265244468)
XLA Ops:
  0.0 15.7 %forward_spectral.1 = (bf16[32,274]{1,0:T(8,128)(2,1)S(1)}, bf16[32,5248]{1,0:T(8,128)(2,1)S(1)}) custom-call(bf16[1,274,5248]{2,1,0:T(8,128)(2,1)} %grid_hbm.1, bf16[1,2,8,640]{3,2,1,0:T(8,128)(2,1)} %bitcast.1, f32[8]{0:T(128)} %gauss_hbm.1, f32[137,137]{1,0:T(8,128)} %modes_hbm.1, f32[137,137]{1,0:T(8,128)} %coupling_hbm.1, f32[137]{0:T(256)} %rates_hbm.1, ...), custom_call_target="tpu_custom_call" | custom-call | tf_op jit(solution)/shard_map/forward_spectral/pallas_call | solution.py:310
  15.7 2.0 %inverse.1 = bf16[1,274,5248]{2,1,0:T(8,128)(2,1)} custom-call(bf16[32,274]{1,0:T(8,128)(2,1)S(1)} %get-tuple-element.7.coef_ref, bf16[32,5248]{1,0:T(8,128)(2,1)S(1)} %get-tuple-element.8.table_ref), custom_call_target="tpu_custom_call" | custom-call | tf_op jit(solution)/shard_map/inverse/pallas_call | solution.py:362
